TPU v7x, 32 devices: a whole 2x2x4 slice. The times are simulated.
32 devices in a mesh: dp: 8 (over z, x), mp: 4 (over y, core).
Axes of the slice: x: 2, y: 2, z: 4, core: 2. Of those that a mesh axis runs over, the one named last changes fastest.
Arguments:
- query_emb: bfloat16 [2048, 768], P('dp'), may hold values from -6 to 6
- positive_list: int32 [2048], replicated, may hold values from 0 to 32767
- centroids: float32 [32768, 768], P(('dp', 'mp')), may hold values from -0.6 to 0.6
- first_moment: float32 [32768, 768], P(('dp', 'mp')), may hold values from -3 to 3
- second_moment: float32 [32768, 768], P(('dp', 'mp')), may hold values from 0.05 to 2
Outputs:
- new_centroids: float32 [32768, 768], P(('dp', 'mp'))
- new_first: float32 [32768, 768], P(('dp', 'mp'))
- new_second: float32 [32768, 768], P(('dp', 'mp'))
- mean_loss: float32 [], replicated
All inputs are finite; a program needn't handle non-finite values.
Results may differ from a plain program's by a relative error of at most 0.00097.
Values may be sent and summed in bfloat16 or wider, within the bound.
A program may use at most 64 MiB of HBM per device.

v0:
```python
import jax
import jax.numpy as jnp
from jax import lax
from jax.sharding import PartitionSpec as P

beta_first = 0.9
beta_second = 0.95
learn_rate = 0.01
epsilon = 1e-08


def adam_update(centroids, first_moment, second_moment, gradient):
    new_first = beta_first * first_moment + (1.0 - beta_first) * gradient
    new_second = beta_second * second_moment + (1.0 - beta_second) * gradient * gradient
    new_centroids = centroids - learn_rate * new_first / (jnp.sqrt(new_second) + epsilon)
    return (new_centroids, new_first, new_second)


def target_logit(logits, is_target):
    return jnp.sum(jnp.where(is_target, logits, jnp.zeros_like(logits)), axis=1)


def row_terms(logits, is_target, row_peak, row_mass, row_target):
    log_norm = row_peak + jnp.log(row_mass)
    row_loss = log_norm - row_target
    weights = (jnp.exp(logits - log_norm[:, None]) - is_target.astype(jnp.float32)).astype(
        jnp.bfloat16
    )
    return (row_loss, weights)


def shards(query_emb, positive_list, centroids, first_moment, second_moment):
    table_half = centroids.astype(jnp.bfloat16)
    own_lists = centroids.shape[0]
    count_mp = lax.axis_size("mp")
    dp_index = lax.axis_index("dp")
    mp_index = lax.axis_index("mp")
    gathered = lax.all_gather(query_emb, "dp", axis=0, tiled=True)
    logits = jnp.einsum("rd,kd->rk", gathered, table_half, preferred_element_type=jnp.float32)
    shard_block = dp_index * count_mp + mp_index
    global_col = shard_block * own_lists + lax.iota(jnp.int32, own_lists)
    is_target = global_col[None, :] == positive_list[:, None]
    row_peak = lax.pmax(jnp.max(logits, axis=1).astype(jnp.bfloat16), ("dp", "mp")).astype(
        jnp.float32
    )
    local_mass = jnp.sum(jnp.exp(logits - row_peak[:, None]), axis=1)
    row_mass, row_target = lax.psum((local_mass, target_logit(logits, is_target)), ("dp", "mp"))
    row_loss, weights = row_terms(logits, is_target, row_peak, row_mass, row_target)
    mean_loss = jnp.mean(row_loss)
    gradient = jnp.einsum("rk,rd->kd", weights, gathered, preferred_element_type=jnp.float32)
    new_centroids, new_first, new_second = adam_update(
        centroids, first_moment, second_moment, gradient
    )
    return (new_centroids, new_first, new_second, mean_loss)


def solution(mesh):
    in_specs = (
        P("dp", None),
        P(),
        P(("dp", "mp"), None),
        P(("dp", "mp"), None),
        P(("dp", "mp"), None),
    )
    out_specs = (P(("dp", "mp"), None), P(("dp", "mp"), None), P(("dp", "mp"), None), P())
    return jax.shard_map(shards, mesh=mesh, in_specs=in_specs, out_specs=out_specs, check_vma=False)
```

profile of v0, /device:TPU:0, one launch (start us, length us, event | category | flops | bytes accessed | tf_op | source)
XLA Modules:
  0.0 188.3 jit_solution(12831864654990041094)
XLA Ops:
  7.2 0.0 all-gather.2.cloned.1.call-start
  7.2 0.7 all-gather.2.cloned.1.call-update
  7.9 0.0 copy-start
  7.9 65.0 %all-gather.2.cloned.1.call-done = bf16[2048,768]{1,0:T(8,128)(2,1)} async-done(((bf16[256,768]{1,0:T(8,128)(2,1)}), bf16[2048,768]{1,0:T(8,128)(2,1)}) %all-gather.2.cloned.1.call-update) | async-done | bytes 3145744 | tf_op jit(solution)/shard_map/all_gather | solution.py:38
  72.9 9.5 %fusion.12 = (bf16[2048]{0:T(1024)(128)(2,1)S(1)}, f32[2048,1024]{0,1:T(8,128)}) fusion(bf16[2048,768]{1,0:T(8,128)(2,1)} %all-gather.2.cloned.1.call-done, f32[1024,768]{1,0:T(8,128)} %param.7), kind=kOutput, calls=%fused_computation.19 | convolution fusion | flops 3224107008 | bytes 14684160 | tf_op jit(solution)/shard_map/rd,kd->rk/dot_general | solution.py:39
  82.4 39.2 %pmax.7 = bf16[2048]{0:T(1024)(128)(2,1)S(1)} all-reduce(bf16[2048]{0:T(1024)(128)(2,1)S(1)} %get-tuple-element.13), channel_id=1, replica_groups=mesh['dp'=8,'mp'=4] {'dp','mp'}, use_global_device_ids=true, to_apply=%region_1.0 | all-reduce | flops 2048 | bytes 8192 | tf_op jit(solution)/shard_map/pmax | solution.py:43
  121.7 0.0 copy-done
  121.7 0.0 copy-start.1
  121.7 4.7 %fusion.2 = (f32[2048]{0:T(1024)S(1)}, f32[2048]{0:T(1024)S(1)}) fusion(f32[2048,1024]{0,1:T(8,128)} %get-tuple-element.14, s32[2048]{0:T(1024)S(1)} %copy-done, s32[1024]{0:T(1024)S(1)} %iota_add_fusion, f32[2048]{0:T(1024)S(1)} %convert_element_type.17), kind=kLoop, calls=%fused_computation.4 | loop fusion | flops 10481664 | bytes 8425472 | tf_op jit(solution)/shard_map/reduce_sum | solution.py:20
  126.4 40.0 %all-reduce = (f32[2048]{0:T(1024)S(1)}, f32[2048]{0:T(1024)S(1)}) all-reduce(f32[2048]{0:T(1024)S(1)} %get-tuple-element.5, f32[2048]{0:T(1024)S(1)} %get-tuple-element.4), channel_id=1, replica_groups=mesh['dp'=8,'mp'=4] {'dp','mp'}, use_global_device_ids=true, to_apply=%region_3.4 | all-reduce | flops 4096 | bytes 32768 | tf_op jit(solution)/shard_map/psum | solution.py:47
  166.5 0.6 subtract_reduce_fusion
  167.8 0.0 copy-done.1
  167.8 12.5 %divide_subtract_fusion = (f32[1024,768]{1,0:T(8,128)}, f32[1024,768]{1,0:T(8,128)}, f32[1024,768]{1,0:T(8,128)}) fusion(f32[1024,768]{1,0:T(8,128)S(1)} %copy-done.1, f32[1024,768]{1,0:T(8,128)} %param.8, f32[1024,768]{1,0:T(8,128)} %param.9, bf16[2048,768]{1,0:T(8,128)(2,1)} %all-gather.2.cloned.1.call-done, f32[2048,1024]{0,1:T(8,128)} %get-tuple-element.14, ...), kind=kOutput, calls=%fused_computation.12 | convolution fusion | flops 3240361984 | bytes 30429184 | tf_op jit(solution)/shard_map/rk,rd->kd/dot_general | solution.py:50
  (2 shorter events, 0.0 us)
Async XLA Ops:
  7.2 65.8 %all-gather.2.cloned.1.call-start = ((), (), s32[]{:S(2)}) async-start(), calls=%async_computation | async-start | bytes 3538944 | tf_op jit(solution)/shard_map/all_gather | solution.py:38
  7.9 113.8 %copy-start = (s32[2048]{0:T(1024)S(1)}, s32[2048]{0:T(1024)}, u32[]{:S(2)}) copy-start(s32[2048]{0:T(1024)} %param.6) | copy-start | bytes 24580
  121.7 46.1 %copy-start.1 = (f32[1024,768]{1,0:T(8,128)S(1)}, f32[1024,768]{1,0:T(8,128)}, u32[]{:S(2)}) copy-start(f32[1024,768]{1,0:T(8,128)} %param.7) | copy-start | bytes 9437188
Sparse Core Ops, SparseCore 0:
  10.2 62.7 all-gather.1
where the time goes:
time: 189 us; the launch traced here: 188 us
  blocking collectives  79.3 us (42%)
  waiting for transfers between devices  65.7 us (35%)
  matrix products  22.1 us (12%)
  between operations  15.8 us (8%)
  other arithmetic  5.35 us (3%)
    all_gather x1, waiting for transfers between devices, shards(): gathered = lax.all_gather(query_emb, 'dp', axis=0, tiled=True)  65 us
    psum x1, blocking collectives, shards(): lax.psum((local_mass, target_logit(logits, is_target)), ('dp', 'mp'))  40 us
    pmax x1, blocking collectives, shards(): lax.pmax(jnp.max(logits, axis=1).astype(jnp.bfloat16), ('dp', 'mp'))  39.2 us
    dot_general x1, matrix products, shards(): jnp.einsum('rk,rd->kd', weights, gathered, preferred_element_type=jnp.flo...  12.5 us
    dot_general x1, matrix products, shards(): jnp.einsum('rd,kd->rk', gathered, table_half, preferred_element_type=jnp....  9.52 us
    reduce_sum x1, other arithmetic, target_logit(): return jnp.sum(jnp.where(is_target, logits, jnp.zeros_like(logits)), axis=1)  4.74 us
  transfers between devices with their start and end apart: 1, of which 1 were waited for; matrix products, arithmetic and copies ran while one was open for 0% of the time, Pallas kernels for 0%

commit v1 on v0

--- a/solution.py
+++ b/solution.py
@@ -44,7 +44,9 @@
         jnp.float32
     )
     local_mass = jnp.sum(jnp.exp(logits - row_peak[:, None]), axis=1)
-    row_mass, row_target = lax.psum((local_mass, target_logit(logits, is_target)), ("dp", "mp"))
+    row_mass, row_target = lax.psum(
+        lax.psum((local_mass, target_logit(logits, is_target)), axis_name="mp"), axis_name="dp"
+    )
     row_loss, weights = row_terms(logits, is_target, row_peak, row_mass, row_target)
     mean_loss = jnp.mean(row_loss)
     gradient = jnp.einsum("rk,rd->kd", weights, gathered, preferred_element_type=jnp.float32)

time: 189 us -> 195 us (1.032)
  blocking collectives: 79.3 us -> 85.9 us
    psum x1 -> x2, blocking collectives: 40 us -> 46.7 us  [the longest x1 35.8 us: shards(): lax.psum(lax.psum((local_mass, target_logit(logits, is_target)), axis_nam...]
where the time goes in v1:
time: 195 us
  blocking collectives  85.9 us (44%)
  waiting for transfers between devices  65.7 us (34%)
  matrix products  22.1 us (11%)
  between operations  15.8 us (8%)
  other arithmetic  5.36 us (3%)
    all_gather x1, waiting for transfers between devices, shards(): gathered = lax.all_gather(query_emb, 'dp', axis=0, tiled=True)  65 us
    pmax x1, blocking collectives, shards(): lax.pmax(jnp.max(logits, axis=1).astype(jnp.bfloat16), ('dp', 'mp'))  39.2 us
    psum x1, blocking collectives, shards(): lax.psum(lax.psum((local_mass, target_logit(logits, is_target)), axis_nam...  35.8 us
    dot_general x1, matrix products, shards(): jnp.einsum('rk,rd->kd', weights, gathered, preferred_element_type=jnp.flo...  12.5 us
    psum x1, blocking collectives, shards(): lax.psum((local_mass, target_logit(logits, is_target)), axis_name='mp')  10.9 us
    dot_general x1, matrix products, shards(): jnp.einsum('rd,kd->rk', gathered, table_half, preferred_element_type=jnp....  9.52 us
    reduce_sum x1, other arithmetic, target_logit(): return jnp.sum(jnp.where(is_target, logits, jnp.zeros_like(logits)), axis=1)  4.74 us
  transfers between devices with their start and end apart: 1, of which 1 were waited for; matrix products, arithmetic and copies ran while one was open for 0% of the time, Pallas kernels for 0%

profile of v1, /device:TPU:0, one launch (start us, length us, event | category | flops | bytes accessed | tf_op | source)
XLA Modules:
  0.0 194.9 jit_solution(18027881691983232604)
XLA Ops:
  7.2 0.0 all-gather.2.cloned.1.call-start
  7.2 0.7 all-gather.2.cloned.1.call-update
  7.9 0.0 copy-start
  7.9 65.0 %all-gather.2.cloned.1.call-done = bf16[2048,768]{1,0:T(8,128)(2,1)} async-done(((bf16[256,768]{1,0:T(8,128)(2,1)}), bf16[2048,768]{1,0:T(8,128)(2,1)}) %all-gather.2.cloned.1.call-update) | async-done | bytes 3145744 | tf_op jit(solution)/shard_map/all_gather | solution.py:38
  72.9 9.5 %fusion.12 = (bf16[2048]{0:T(1024)(128)(2,1)S(1)}, f32[2048,1024]{0,1:T(8,128)}) fusion(bf16[2048,768]{1,0:T(8,128)(2,1)} %all-gather.2.cloned.1.call-done, f32[1024,768]{1,0:T(8,128)} %param.7), kind=kOutput, calls=%fused_computation.19 | convolution fusion | flops 3224107008 | bytes 14684160 | tf_op jit(solution)/shard_map/rd,kd->rk/dot_general | solution.py:39
  82.4 39.2 %pmax.7 = bf16[2048]{0:T(1024)(128)(2,1)S(1)} all-reduce(bf16[2048]{0:T(1024)(128)(2,1)S(1)} %get-tuple-element.15), channel_id=1, replica_groups=mesh['dp'=8,'mp'=4] {'dp','mp'}, use_global_device_ids=true, to_apply=%region_1.0 | all-reduce | flops 2048 | bytes 8192 | tf_op jit(solution)/shard_map/pmax | solution.py:43
  121.7 0.0 copy-done
  121.7 0.0 copy-start.1
  121.7 4.7 %fusion.2 = (f32[2048]{0:T(1024)S(1)}, f32[2048]{0:T(1024)S(1)}) fusion(f32[2048,1024]{0,1:T(8,128)} %get-tuple-element.16, s32[2048]{0:T(1024)S(1)} %copy-done, s32[1024]{0:T(1024)S(1)} %iota_add_fusion, f32[2048]{0:T(1024)S(1)} %convert_element_type.17), kind=kLoop, calls=%fused_computation.4 | loop fusion | flops 10481664 | bytes 8425472 | tf_op jit(solution)/shard_map/reduce_sum | solution.py:20
  126.4 10.9 %all-reduce.1 = (f32[2048]{0:T(1024)S(1)}, f32[2048]{0:T(1024)S(1)}) all-reduce(f32[2048]{0:T(1024)S(1)} %get-tuple-element.5, f32[2048]{0:T(1024)S(1)} %get-tuple-element.4), channel_id=1, replica_groups=mesh['dp'=8,'mp'=4] {'mp'}, use_global_device_ids=true, to_apply=%region_3.4 | all-reduce | flops 4096 | bytes 32768 | tf_op jit(solution)/shard_map/psum | solution.py:48
  137.4 35.8 %all-reduce = (f32[2048]{0:T(1024)S(1)}, f32[2048]{0:T(1024)S(1)}) all-reduce(f32[2048]{0:T(1024)S(1)} %get-tuple-element.8, f32[2048]{0:T(1024)S(1)} %get-tuple-element.9), channel_id=1, replica_groups=mesh['dp'=8,'mp'=4] {'dp'}, use_global_device_ids=true, to_apply=%region_4.5 | all-reduce | flops 4096 | bytes 32768 | tf_op jit(solution)/shard_map/psum | solution.py:47
  173.1 0.6 subtract_reduce_fusion
  174.4 0.0 copy-done.1
  174.4 12.5 %divide_subtract_fusion = (f32[1024,768]{1,0:T(8,128)}, f32[1024,768]{1,0:T(8,128)}, f32[1024,768]{1,0:T(8,128)}) fusion(f32[1024,768]{1,0:T(8,128)S(1)} %copy-done.1, f32[1024,768]{1,0:T(8,128)} %param.8, f32[1024,768]{1,0:T(8,128)} %param.9, bf16[2048,768]{1,0:T(8,128)(2,1)} %all-gather.2.cloned.1.call-done, f32[2048,1024]{0,1:T(8,128)} %get-tuple-element.16, ...), kind=kOutput, calls=%fused_computation.12 | convolution fusion | flops 3240361984 | bytes 30429184 | tf_op jit(solution)/shard_map/rk,rd->kd/dot_general | solution.py:52
  (2 shorter events, 0.0 us)
Async XLA Ops:
  7.2 65.8 %all-gather.2.cloned.1.call-start = ((), (), s32[]{:S(2)}) async-start(), calls=%async_computation | async-start | bytes 3538944 | tf_op jit(solution)/shard_map/all_gather | solution.py:38
  7.9 113.8 %copy-start = (s32[2048]{0:T(1024)S(1)}, s32[2048]{0:T(1024)}, u32[]{:S(2)}) copy-start(s32[2048]{0:T(1024)} %param.6) | copy-start | bytes 24580
  121.7 52.7 %copy-start.1 = (f32[1024,768]{1,0:T(8,128)S(1)}, f32[1024,768]{1,0:T(8,128)}, u32[]{:S(2)}) copy-start(f32[1024,768]{1,0:T(8,128)} %param.7) | copy-start | bytes 9437188
Sparse Core Ops, SparseCore 0:
  10.2 62.7 all-gather.1
